TPU v7x, 128 devices: a whole 4x4x4 slice. The times are simulated.
128 devices in a mesh: owner: 8 (over x, core), rows: 16 (over z, y).
Axes of the slice: x: 4, y: 4, z: 4, core: 2. Of those that a mesh axis runs over, the one named last changes fastest.
Arguments:
- master_gate: float32 [64, 2048, 1024], P('owner', 'rows'), may hold values from -0.1875 to 0.1875
- second_gate: bfloat16 [64, 2048, 1024], P('owner', 'rows'), may hold values from -0.0625 to 0.0625
- master_up: float32 [64, 2048, 1024], P('owner', 'rows'), may hold values from -0.1875 to 0.1875
- second_up: bfloat16 [64, 2048, 1024], P('owner', 'rows'), may hold values from -0.0625 to 0.0625
- master_down: float32 [64, 1024, 2048], P('owner', None, 'rows'), may hold values from -0.25 to 0.25
- second_down: bfloat16 [64, 1024, 2048], P('owner', None, 'rows'), may hold values from -0.09375 to 0.09375
- router_weight: float32 [2048, 64], P('rows', 'owner'), may hold values from -0.125 to 0.125
- router_gain: float32 [2048], P('rows'), may hold values from 0.25 to 1.75
Outputs:
- final_gate: bfloat16 [64, 2048, 1024], P('owner', None, 'rows')
- final_up: bfloat16 [64, 2048, 1024], P('owner', None, 'rows')
- final_down: bfloat16 [64, 1024, 2048], P('owner', 'rows')
- scale_gate: float32 [64, 1024], P('owner', 'rows')
- scale_up: float32 [64, 1024], P('owner', 'rows')
- scale_down: float32 [64, 1024], P('owner', 'rows')
- serve_router: bfloat16 [2048, 64], replicated
All inputs are finite; a program needn't handle non-finite values.
Results may differ from a plain program's by a relative error of at most 0.001.
Values may be sent and summed in bfloat16 or wider, within the bound.
A program may use at most 128 MiB of HBM per device.

v0:
```python
import jax
import jax.numpy as jnp
from jax import lax
from jax.sharding import PartitionSpec as P


def sent_to_all(shard, axis):
    copies = jnp.broadcast_to(shard, (lax.axis_size(axis), *shard.shape))
    return lax.all_to_all(copies, axis, split_axis=0, concat_axis=0, tiled=True)


def taken_together(shard, axis):
    return sent_to_all(shard, axis).sum(axis=0)


def together(arrays, axis):
    ravelled, at, done = (jnp.concatenate([a.reshape(-1) for a in arrays]), 0, [])
    so_far = taken_together(ravelled, axis)
    for a in arrays:
        done.append(so_far[at : at + a.size].reshape(a.shape))
        at += a.size
    return tuple(done)


def side_by_side(arrays, axis, split_dim, concat_dim, along):
    both = jnp.concatenate(arrays, axis=along)
    result, at, done = (
        lax.all_to_all(both, axis, split_axis=split_dim, concat_axis=concat_dim, tiled=True),
        0,
        [],
    )
    for a in arrays:
        done.append(lax.slice_in_dim(result, at, at + a.shape[along], axis=along))
        at += a.shape[along]
    return tuple(done)


def split_up(shard, dim, peers):
    before, after = (shard.shape[:dim], shard.shape[dim + 1 :])
    return jnp.moveaxis(shard.reshape(*before, peers, -1, *after), dim, 0)


def piece_ends(length, count):
    unit = 8 if length >= 8 * count else 1
    return [length // unit * k // count * unit for k in range(1, count)]


def laid_out(blocks, dim):
    blocks = jnp.moveaxis(blocks, 0, dim)
    shape = blocks.shape
    return blocks.reshape(*shape[:dim], shape[dim] * shape[dim + 1], *shape[dim + 2 :])


def several_exchanges(shard, axis, pieces, split_dim, concat_dim):
    blocks = split_up(shard, split_dim, lax.axis_size(axis))
    cut = max(range(1, max(2, blocks.ndim - 1)), key=lambda d: blocks.shape[d])
    done = []
    for share in jnp.split(blocks, piece_ends(blocks.shape[cut], pieces), axis=cut):
        if share.size:
            done.append(lax.all_to_all(share, axis, split_axis=0, concat_axis=0, tiled=True))
    return laid_out(jnp.concatenate(done, axis=cut), concat_dim)


def gather_directly(shard, axis, dim):
    blocks = sent_to_all(shard, axis)
    return laid_out(blocks, dim)


def body(
    master_gate,
    second_gate,
    master_up,
    second_up,
    master_down,
    second_down,
    router_weight,
    router_gain,
):
    merged_gate = master_gate + second_gate.astype(jnp.float32)
    merged_up = master_up + second_up.astype(jnp.float32)
    merged_down = master_down + second_down.astype(jnp.float32)
    total_gate, total_up, total_down = together(
        (
            jnp.sum(merged_gate * merged_gate, axis=1),
            jnp.sum(merged_up * merged_up, axis=1),
            jnp.sum(merged_down * merged_down, axis=2),
        ),
        "rows",
    )
    scale_gate = jnp.sqrt(total_gate)
    scale_up = jnp.sqrt(total_up)
    scale_down = jnp.sqrt(total_down)
    narrow_gate, narrow_up, narrow_down = (
        (merged_gate / jnp.expand_dims(scale_gate, 1)).astype(jnp.bfloat16),
        (merged_up / jnp.expand_dims(scale_up, 1)).astype(jnp.bfloat16),
        (merged_down / jnp.expand_dims(scale_down, 2)).astype(jnp.bfloat16),
    )
    final_gate, final_up = side_by_side((narrow_gate, narrow_up), "rows", 2, 1, 0)
    final_down = several_exchanges(narrow_down, "rows", 2, 1, 2)
    scale_gate = lax.dynamic_slice_in_dim(
        scale_gate, lax.axis_index("rows") * final_gate.shape[2], final_gate.shape[2], axis=1
    )
    scale_up = lax.dynamic_slice_in_dim(
        scale_up, lax.axis_index("rows") * final_up.shape[2], final_up.shape[2], axis=1
    )
    scale_down = lax.dynamic_slice_in_dim(
        scale_down, lax.axis_index("rows") * final_down.shape[1], final_down.shape[1], axis=1
    )
    part_router = (router_weight * router_gain[:, None]).astype(jnp.bfloat16)
    row_router = gather_directly(part_router, "rows", 0)
    serve_router = gather_directly(row_router, "owner", 1)
    return (final_gate, final_up, final_down, scale_gate, scale_up, scale_down, serve_router)


def solution(mesh):
    placed = (
        P("owner", "rows", None),
        P("owner", "rows", None),
        P("owner", "rows", None),
        P("owner", "rows", None),
        P("owner", None, "rows"),
        P("owner", None, "rows"),
        P("rows", "owner"),
        P("rows"),
    )
    return jax.shard_map(
        body,
        mesh=mesh,
        in_specs=placed,
        out_specs=(
            P("owner", None, "rows"),
            P("owner", None, "rows"),
            P("owner", "rows", None),
            P("owner", "rows"),
            P("owner", "rows"),
            P("owner", "rows"),
            P(),
        ),
        check_vma=False,
    )
```

profile of v0, /device:TPU:0, one launch (start us, length us, event | category | flops | bytes accessed | tf_op | source)
XLA Modules:
  0.0 202.4 jit_solution(13047169059968651824)
XLA Ops:
  1.9 8.2 %all-to-all-start.4 = ((bf16[16,128,8]{1,2,0:T(8,128)(2,1)}), bf16[16,128,8]{1,2,0:T(8,128)(2,1)S(1)}, u32[]{:S(2)}, u32[]{:S(2)}) async-start(bf16[16,128,8]{1,2,0:T(8,128)(2,1)} %broadcast_in_dim.14), calls=%async_computation.4 | async-start | bytes 65536 | tf_op jit(solution)/shard_map/all_to_all | solution.py:9
  10.1 5.4 %copy.94 = f32[8,128,1024]{1,0,2:T(8,128)} copy(f32[8,128,1024]{2,1,0:T(8,128)} %param.10) | data formatting | bytes 8388608 | tf_op args[2]
  15.5 3.4 %copy.93 = bf16[8,128,1024]{1,0,2:T(8,128)(2,1)S(1)} copy(bf16[8,128,1024]{2,1,0:T(8,128)(2,1)} %param.11) | data formatting | bytes 4194304 | tf_op args[3]
  18.9 3.4 %multiply_reduce_fusion.1 = f32[8,1024]{0,1:T(8,128)S(1)} fusion(f32[8,128,1024]{1,0,2:T(8,128)} %copy.94, bf16[8,128,1024]{1,0,2:T(8,128)(2,1)S(1)} %copy.93), kind=kLoop, calls=%fused_computation.6 | loop fusion | flops 4186112 | bytes 6324224 | tf_op jit(solution)/shard_map/reduce_sum | solution.py:85
  22.4 5.4 %copy.91 = f32[8,128,1024]{1,0,2:T(8,128)} copy(f32[8,128,1024]{2,1,0:T(8,128)} %param.8) | data formatting | bytes 8388608 | tf_op args[0]
  27.8 4.1 %copy.90 = bf16[8,128,1024]{1,0,2:T(8,128)(2,1)} copy(bf16[8,128,1024]{2,1,0:T(8,128)(2,1)} %param.9) | data formatting | bytes 4194304 | tf_op args[1]
  32.0 4.1 %multiply_reduce_fusion.2 = f32[8,1024]{0,1:T(8,128)S(1)} fusion(f32[8,128,1024]{1,0,2:T(8,128)} %copy.91, bf16[8,128,1024]{1,0,2:T(8,128)(2,1)} %copy.90), kind=kLoop, calls=%fused_computation.8 | loop fusion | flops 4186112 | bytes 6324224 | tf_op jit(solution)/shard_map/reduce_sum | solution.py:84
  36.2 4.0 %multiply_reduce_fusion = f32[8,1024]{1,0:T(8,128)S(1)} fusion(f32[8,1024,128]{2,1,0:T(8,128)} %param.12, bf16[8,1024,128]{2,1,0:T(8,128)(2,1)} %param.13), kind=kLoop, calls=%fused_computation.4 | loop fusion | flops 4186112 | bytes 6324224 | tf_op jit(solution)/shard_map/reduce_sum | solution.py:86
  40.3 1.2 broadcast_in_dim.6
  41.5 29.4 %all_to_all.41 = f32[16,1,24576]{2,1,0:T(1,128)} all-to-all(f32[16,1,24576]{2,1,0:T(1,128)S(1)} %broadcast_in_dim.6), channel_id=1, replica_groups=mesh['owner'=8,'rows'=16] {'rows'}, dimensions={0} | all-to-all | bytes 3145728 | tf_op jit(solution)/shard_map/all_to_all | solution.py:9
  71.6 4.3 %all-to-all-start.5 = ((bf16[8,2048,8]{1,2,0:T(8,128)(2,1)}), bf16[8,2048,8]{1,2,0:T(8,128)(2,1)S(1)}, u32[]{:S(2)}, u32[]{:S(2)}) async-start(bf16[8,2048,8]{1,2,0:T(8,128)(2,1)} %broadcast_in_dim.15), calls=%async_computation.5 | async-start | bytes 524288 | tf_op jit(solution)/shard_map/all_to_all | solution.py:9
  75.9 2.4 %reduce_sum.39 = f32[24576]{0:T(1024)S(1)} reduce(f32[16,1,24576]{2,1,0:T(1,128)} %all_to_all.41, f32[]{:T(128)} %constant.5.clone.1), dimensions={0,1}, to_apply=%region_3.0 | reduce | flops 368640 | bytes 1671172 | tf_op jit(solution)/shard_map/reduce_sum | solution.py:13
  78.4 3.4 %divide_convert_fusion = bf16[8,1024,128]{2,1,0:T(8,128)(2,1)S(1)} fusion(f32[8,1024,128]{2,1,0:T(8,128)} %param.12, bf16[8,1024,128]{2,1,0:T(8,128)(2,1)} %param.13, f32[8,1024]{1,0:T(8,128)S(1)} %sqrt.23), kind=kLoop, calls=%fused_computation.1 | loop fusion | flops 4194304 | bytes 8421376 | tf_op jit(solution)/shard_map/convert_element_type | solution.py:96
  81.8 1.3 fusion
  83.2 1.2 copy.102
  84.3 3.7 %all-to-all-start.2 = ((bf16[16,8,32,128]{3,2,1,0:T(8,128)(2,1)}), bf16[16,8,32,128]{3,2,1,0:T(8,128)(2,1)S(1)}, u32[]{:S(2)}, u32[]{:S(2)}) async-start(bf16[16,8,32,128]{3,2,1,0:T(8,128)(2,1)} %copy.102), calls=%async_computation.2 | async-start | bytes 2097152 | tf_op jit(solution)/shard_map/all_to_all | solution.py:60
  88.0 1.0 copy.97
  89.0 2.3 %copy.103 = bf16[16,8,32,128]{3,2,1,0:T(8,128)(2,1)} copy(bf16[16,8,32,128]{3,2,0,1:T(8,128)(2,1)} %get-tuple-element.10) | data formatting | bytes 2097152 | tf_op jit(solution)/shard_map/split | solution.py:58
  91.3 16.3 %all-to-all-done.2 = bf16[16,8,32,128]{3,2,1,0:T(8,128)(2,1)S(1)} async-done(((bf16[16,8,32,128]{3,2,1,0:T(8,128)(2,1)}), bf16[16,8,32,128]{3,2,1,0:T(8,128)(2,1)S(1)}, u32[]{:S(2)}, u32[]{:S(2)}) %all-to-all-start.2) | async-done | bytes 1048608 | tf_op jit(solution)/shard_map/all_to_all | solution.py:60
  107.6 4.5 %all-to-all-start.3 = ((bf16[16,8,32,128]{3,2,1,0:T(8,128)(2,1)}), bf16[16,8,32,128]{3,2,1,0:T(8,128)(2,1)}, u32[]{:S(2)}, u32[]{:S(2)}) async-start(bf16[16,8,32,128]{3,2,1,0:T(8,128)(2,1)} %copy.103), calls=%async_computation.3 | async-start | bytes 2097152 | tf_op jit(solution)/shard_map/all_to_all | solution.py:60
  112.2 4.6 %divide_convert_fusion.2 = bf16[8,128,1024]{1,0,2:T(8,128)(2,1)} fusion(f32[8,128,1024]{1,0,2:T(8,128)} %copy.91, bf16[8,128,1024]{1,0,2:T(8,128)(2,1)} %copy.90, f32[8,1024]{0,1:T(8,128)} %copy.97), kind=kLoop, calls=%fused_computation.3 | loop fusion | flops 4194304 | bytes 8421376 | tf_op jit(solution)/shard_map/convert_element_type | solution.py:94
  116.7 1.0 copy.98
  117.8 4.1 %divide_convert_fusion.1 = bf16[8,128,1024]{1,0,2:T(8,128)(2,1)S(1)} fusion(f32[8,128,1024]{1,0,2:T(8,128)} %copy.94, bf16[8,128,1024]{1,0,2:T(8,128)(2,1)S(1)} %copy.93, f32[8,1024]{0,1:T(8,128)} %copy.98), kind=kLoop, calls=%fused_computation.2 | loop fusion | flops 4194304 | bytes 8421376 | tf_op jit(solution)/shard_map/convert_element_type | solution.py:95
  121.9 2.7 %pad_maximum_fusion = bf16[16,128,1024]{1,0,2:T(8,128)(2,1)} fusion(bf16[8,128,1024]{1,0,2:T(8,128)(2,1)S(1)} %divide_convert_fusion.1, bf16[8,128,1024]{1,0,2:T(8,128)(2,1)S(1)} %copy-done), kind=kLoop, calls=%fused_computation | loop fusion | flops 8388608 | bytes 8388608 | tf_op jit(solution)/shard_map/concatenate | solution.py:26
  124.6 5.2 %all-to-all-done.3 = bf16[16,8,32,128]{3,2,1,0:T(8,128)(2,1)} async-done(((bf16[16,8,32,128]{3,2,1,0:T(8,128)(2,1)}), bf16[16,8,32,128]{3,2,1,0:T(8,128)(2,1)}, u32[]{:S(2)}, u32[]{:S(2)}) %all-to-all-start.3) | async-done | bytes 1048608 | tf_op jit(solution)/shard_map/all_to_all | solution.py:60
  129.8 4.5 %all-to-all-start.1 = ((bf16[16,128,1024]{1,0,2:T(8,128)(2,1)}), bf16[16,128,1024]{1,0,2:T(8,128)(2,1)}, u32[]{:S(2)}, u32[]{:S(2)}) async-start(bf16[16,128,1024]{1,0,2:T(8,128)(2,1)} %pad_maximum_fusion), calls=%async_computation.1 | async-start | bytes 8388608 | tf_op jit(solution)/shard_map/all_to_all | solution.py:28
  136.3 2.9 %copy_bitcast_fusion = bf16[8,64,2048]{2,1,0:T(8,128)(2,1)} fusion(bf16[16,8,32,128]{3,2,1,0:T(8,128)(2,1)} %all-to-all-done.3, bf16[16,8,32,128]{3,2,1,0:T(8,128)(2,1)S(1)} %all-to-all-done.2), kind=kLoop, calls=%fused_computation.10 | loop fusion | flops 4194304 | bytes 4194304 | tf_op jit(solution)/shard_map/reshape | solution.py:51
  139.2 54.5 %all-to-all-done.1 = bf16[16,128,1024]{1,0,2:T(8,128)(2,1)} async-done(((bf16[16,128,1024]{1,0,2:T(8,128)(2,1)}), bf16[16,128,1024]{1,0,2:T(8,128)(2,1)}, u32[]{:S(2)}, u32[]{:S(2)}) %all-to-all-start.1) | async-done | bytes 4194336 | tf_op jit(solution)/shard_map/all_to_all | solution.py:28
  193.7 3.3 %copy.99 = bf16[16,128,1024]{1,2,0:T(8,128)(2,1)S(1)} copy(bf16[16,128,1024]{1,0,2:T(8,128)(2,1)} %all-to-all-done.1) | data formatting | bytes 8388608 | tf_op jit(solution)/shard_map/all_to_all | solution.py:28
  197.0 1.0 slice_bitcast_fusion
  198.0 1.9 copy.121
  199.8 1.9 copy.122
  (20 shorter events, 5.2 us)
Async XLA Ops:
  1.9 38.3 %all-to-all-start.4 = ((bf16[16,128,8]{1,2,0:T(8,128)(2,1)}), bf16[16,128,8]{1,2,0:T(8,128)(2,1)S(1)}, u32[]{:S(2)}, u32[]{:S(2)}) async-start(bf16[16,128,8]{1,2,0:T(8,128)(2,1)} %broadcast_in_dim.14), calls=%async_computation.4 | async-start | bytes 65536 | tf_op jit(solution)/shard_map/all_to_all | solution.py:9
  71.6 12.7 %all-to-all-start.5 = ((bf16[8,2048,8]{1,2,0:T(8,128)(2,1)}), bf16[8,2048,8]{1,2,0:T(8,128)(2,1)S(1)}, u32[]{:S(2)}, u32[]{:S(2)}) async-start(bf16[8,2048,8]{1,2,0:T(8,128)(2,1)} %broadcast_in_dim.15), calls=%async_computation.5 | async-start | bytes 524288 | tf_op jit(solution)/shard_map/all_to_all | solution.py:9
  84.3 23.3 %all-to-all-start.2 = ((bf16[16,8,32,128]{3,2,1,0:T(8,128)(2,1)}), bf16[16,8,32,128]{3,2,1,0:T(8,128)(2,1)S(1)}, u32[]{:S(2)}, u32[]{:S(2)}) async-start(bf16[16,8,32,128]{3,2,1,0:T(8,128)(2,1)} %copy.102), calls=%async_computation.2 | async-start | bytes 2097152 | tf_op jit(solution)/shard_map/all_to_all | solution.py:60
  107.6 22.1 %all-to-all-start.3 = ((bf16[16,8,32,128]{3,2,1,0:T(8,128)(2,1)}), bf16[16,8,32,128]{3,2,1,0:T(8,128)(2,1)}, u32[]{:S(2)}, u32[]{:S(2)}) async-start(bf16[16,8,32,128]{3,2,1,0:T(8,128)(2,1)} %copy.103), calls=%async_computation.3 | async-start | bytes 2097152 | tf_op jit(solution)/shard_map/all_to_all | solution.py:60
  117.7 4.1 %copy-start = (bf16[8,128,1024]{1,0,2:T(8,128)(2,1)S(1)}, bf16[8,128,1024]{1,0,2:T(8,128)(2,1)}, u32[]{:S(2)}) copy-start(bf16[8,128,1024]{1,0,2:T(8,128)(2,1)} %divide_convert_fusion.2) | copy-start | bytes 6291460
  129.8 63.9 %all-to-all-start.1 = ((bf16[16,128,1024]{1,0,2:T(8,128)(2,1)}), bf16[16,128,1024]{1,0,2:T(8,128)(2,1)}, u32[]{:S(2)}, u32[]{:S(2)}) async-start(bf16[16,128,1024]{1,0,2:T(8,128)(2,1)} %pad_maximum_fusion), calls=%async_computation.1 | async-start | bytes 8388608 | tf_op jit(solution)/shard_map/all_to_all | solution.py:28
where the time goes:
time: 203 us; the launch traced here: 202 us
  waiting for transfers between devices  76.1 us (37%)
  local copies, waits for them, and re-layouts  38.8 us (19%)
  other arithmetic  32.3 us (16%)
  blocking collectives  29.4 us (14%)
  starting transfers between devices  25.2 us (12%)
    all_to_all x1, waiting for transfers between devices, side_by_side(): lax.all_to_all(both, axis, split_axis=split_dim, concat_axis=concat_dim,...  54.5 us
    all_to_all x1, blocking collectives, sent_to_all(): return lax.all_to_all(copies, axis, split_axis=0, concat_axis=0, tiled=True)  29.4 us
    all_to_all x2, waiting for transfers between devices, several_exchanges(): lax.all_to_all(share, axis, split_axis=0, concat_axis=0, tiled=True)  21.5 us
    unnamed x9, local copies, waits for them, and re-layouts  20 us
    all_to_all x2, starting transfers between devices, sent_to_all(): return lax.all_to_all(copies, axis, split_axis=0, concat_axis=0, tiled=True)  12.5 us
    all_to_all x2, starting transfers between devices, several_exchanges(): lax.all_to_all(share, axis, split_axis=0, concat_axis=0, tiled=True)  8.17 us
    split x3, local copies, waits for them, and re-layouts, several_exchanges(): jnp.split(blocks, piece_ends(blocks.shape[cut], pieces), axis=cut)  4.8 us
    convert_element_type x1, other arithmetic, body(): (merged_gate / jnp.expand_dims(scale_gate, 1)).astype(jnp.bfloat16)  4.56 us
  transfers between devices with their start and end apart: 5, of which 3 were waited for; matrix products, arithmetic and copies ran while one was open for 29% of the time, Pallas kernels for 0%

commit v1 on v0

v1 whole, which is shorter than its diff:
```python
import functools

import jax
import jax.numpy as jnp
from jax import lax
from jax.experimental import pallas as pl
from jax.experimental.pallas import tpu as pltpu
from jax.sharding import PartitionSpec as P

F32 = jnp.float32
BF16 = jnp.bfloat16
MESH = pl.DeviceIdType.MESH
Y = 4
LANES = 128


def exchange_kernel(
    rows,
    owners,
    mg, sg, mu, su, md, sd, rw, gain,
    og, ou, od, sc, ro,
    vmg, vsg, vmu, vsu, vmd, vsd, vrw, vgain,
    send, ps, rb, tt,
    in_sem, small_sem, stat_send, stat_recv, tot_send, tot_recv,
    data_send, data_recv, row_send, row_recv, own_send, own_recv,
):
    experts = mg.shape[0]
    width = mg.shape[2]
    blocks = width // LANES
    mine = width // rows
    halves = rows // blocks
    part = experts // halves
    owner = lax.axis_index("owner")
    me = lax.axis_index("rows")
    z, y = me // Y, me % Y
    peers = [((z + k // Y) % (rows // Y)) * Y + (y + k % Y) % Y for k in range(1, rows)]
    others = [(owner + k) % owners for k in range(1, owners)]

    barrier = pltpu.get_barrier_semaphore()
    for p in peers:
        pl.semaphore_signal(barrier, inc=1, device_id={"rows": p}, device_id_type=MESH)
    for p in others:
        pl.semaphore_signal(barrier, inc=1, device_id={"owner": p}, device_id_type=MESH)

    matrices = (
        (mg, sg, vmg, vsg, og, True),
        (mu, su, vmu, vsu, ou, True),
        (md, sd, vmd, vsd, od, False),
    )

    def loads(m, e):
        master, second, vm, vs = matrices[m][:4]
        return (
            pltpu.make_async_copy(master.at[e], vm.at[e], in_sem.at[2 * m, e]),
            pltpu.make_async_copy(second.at[e], vs.at[e], in_sem.at[2 * m + 1, e]),
        )

    for m in range(3):
        @pl.loop(0, experts)
        def _(e):
            for c in loads(m, e):
                c.start()

    small = (
        pltpu.make_async_copy(rw, vrw, small_sem.at[0]),
        pltpu.make_async_copy(gain, vgain, small_sem.at[1]),
    )
    for c in small:
        c.start()

    for m in range(3):
        vm, vs, across = matrices[m][2], matrices[m][3], matrices[m][5]

        @pl.loop(0, experts)
        def _(e):
            for c in loads(m, e):
                c.wait()
            half, at = e // part, m * part + e % part
            if across:
                acc = jnp.zeros((8, width), F32)
                for i in range(0, vm.shape[1], 16):
                    x = vm[e, i : i + 16, :] + vs[e, i : i + 16, :].astype(F32)
                    x = x * x
                    acc = acc + x[:8] + x[8:]
                total = jnp.sum(acc, axis=0, keepdims=True)
                for b in range(blocks):
                    ps[half, b, pl.ds(at, 1), :] = total[:, b * LANES : (b + 1) * LANES]
            else:
                for b in range(blocks):
                    x = vm[e, b * LANES : (b + 1) * LANES, :] + vs[e, b * LANES : (b + 1) * LANES, :].astype(F32)
                    ps[half, b, pl.ds(at, 1), :] = jnp.sum((x * x).T, axis=0, keepdims=True)

    pl.semaphore_wait(barrier, rows - 1 + owners - 1)

    def stat_copy(p):
        return pltpu.make_async_remote_copy(
            src_ref=ps.at[p // blocks, p % blocks], dst_ref=rb.at[me],
            send_sem=stat_send, recv_sem=stat_recv, device_id={"rows": p}, device_id_type=MESH,
        )

    for p in peers:
        stat_copy(p).start()
    rb[me] = ps[me // blocks, me % blocks]

    lanes = pl.ds(pl.multiple_of(me * LANES, LANES), LANES)
    for c in small:
        c.wait()
    ro[owner, :, lanes] = (vrw[...] * vgain[...]).astype(BF16)

    def row_copy(p):
        return pltpu.make_async_remote_copy(
            src_ref=ro.at[owner, :, lanes], dst_ref=ro.at[owner, :, lanes],
            send_sem=row_send, recv_sem=row_recv, device_id={"rows": p}, device_id_type=MESH,
        )

    for p in peers:
        row_copy(p).start()

    others_rb = rb.at[pl.ds(0, rows - 1)]
    pltpu.make_async_copy(others_rb, others_rb, stat_recv).wait()
    total = rb[0]
    for k in range(1, rows):
        total = total + rb[k]
    tt[me // blocks, me % blocks] = total

    def total_copy(p):
        here = tt.at[me // blocks, me % blocks]
        return pltpu.make_async_remote_copy(
            src_ref=here, dst_ref=here,
            send_sem=tot_send, recv_sem=tot_recv, device_id={"rows": p}, device_id_type=MESH,
        )

    for p in peers:
        total_copy(p).start()
    pltpu.make_async_copy(others_rb, others_rb, tot_recv).wait()

    def data_copy(m, e, p):
        return pltpu.make_async_remote_copy(
            src_ref=send.at[m, e, pl.ds(pl.multiple_of(p * mine, mine), mine)],
            dst_ref=matrices[m][4].at[e, :, lanes],
            send_sem=data_send.at[m], recv_sem=data_recv.at[m],
            device_id={"rows": p}, device_id_type=MESH,
        )

    def own_copy(p):
        return pltpu.make_async_remote_copy(
            src_ref=ro.at[owner], dst_ref=ro.at[owner],
            send_sem=own_send, recv_sem=own_recv, device_id={"owner": p}, device_id_type=MESH,
        )

    for m in range(3):
        vm, vs, out, across = matrices[m][2], matrices[m][3], matrices[m][4], matrices[m][5]

        @pl.loop(0, experts)
        def _(e):
            half, at = e // part, m * part + e % part
            for b in range(blocks):
                sl = slice(b * LANES, (b + 1) * LANES)
                inverse = 1.0 / jnp.sqrt(tt[half, b, pl.ds(at, 1), :])
                if across:
                    x = (vm[e, :, sl] + vs[e, :, sl].astype(F32)) * inverse
                    send[m, e, sl, :] = x.T.astype(BF16)
                else:
                    x = vm[e, sl, :] + vs[e, sl, :].astype(F32)
                    send[m, e, sl, :] = (x * jnp.broadcast_to(inverse, (LANES, LANES)).T).astype(BF16)
            for p in peers:
                data_copy(m, e, p).start()
            out[e, :, lanes] = send[m, e, pl.ds(pl.multiple_of(me * mine, mine), mine), :]

        if m == 0:
            arrived = ro.at[owner, :, pl.ds(0, (rows - 1) * LANES)]
            pltpu.make_async_copy(arrived, arrived, row_recv).wait()
            pltpu.make_async_copy(arrived, arrived, row_send).wait()
            for p in others:
                own_copy(p).start()

    for m in range(3):
        for h in range(halves):
            s = jnp.sqrt(tt[h, me // 2, m * part : (m + 1) * part, :])
            s = jnp.where(me % 2 == 1, pltpu.roll(s, LANES - mine, 1), s)
            sc[m, h * part : (h + 1) * part, :] = s[:, :mine]

    pltpu.make_async_copy(others_rb, others_rb, stat_send).wait()
    pltpu.make_async_copy(others_rb, others_rb, tot_send).wait()
    theirs = ro.at[pl.ds(0, owners - 1)]
    pltpu.make_async_copy(theirs, theirs, own_send).wait()
    pltpu.make_async_copy(theirs, theirs, own_recv).wait()
    for m in range(3):
        sent = send.at[m, :, pl.ds(0, (rows - 1) * mine), :]
        pltpu.make_async_copy(sent, sent, data_send.at[m]).wait()
        pltpu.make_async_copy(sent, sent, data_recv.at[m]).wait()


def store_kernel(og, ou, od, sc, ro, fg, fu, fd, a, b, c, fr, sem):
    copies = [
        pltpu.make_async_copy(og, fg, sem.at[0]),
        pltpu.make_async_copy(ou, fu, sem.at[1]),
        pltpu.make_async_copy(od, fd, sem.at[2]),
        pltpu.make_async_copy(ro, fr, sem.at[3]),
        pltpu.make_async_copy(sc.at[0], a, sem.at[4]),
        pltpu.make_async_copy(sc.at[1], b, sem.at[5]),
        pltpu.make_async_copy(sc.at[2], c, sem.at[6]),
    ]
    for copy in copies:
        copy.start()
    for copy in copies:
        copy.wait()


def solution(mesh):
    owners, rows = mesh.shape["owner"], mesh.shape["rows"]

    def body(mg, sg, mu, su, md, sd, rw, gain):
        experts, deep, width = mg.shape
        blocks = width // LANES
        halves = rows // blocks
        units = 3 * experts // halves
        mine = width // rows
        hbm = pl.BlockSpec(memory_space=pltpu.HBM)
        vmem = pl.BlockSpec(memory_space=pltpu.VMEM)
        result = pltpu.VMEM((experts, mine, rows * LANES), BF16)
        args = [mg, sg, mu, su, md, sd, rw.T, gain[None, :]]
        args = [pltpu.with_memory_space_constraint(x, pltpu.HBM) for x in args]
        og, ou, od, sc, ro = pl.pallas_call(
            functools.partial(exchange_kernel, rows, owners),
            out_shape=[
                result, result, result,
                pltpu.VMEM((3, experts, mine), F32),
                pltpu.VMEM((owners, rw.shape[1], rows * LANES), BF16),
            ],
            in_specs=[hbm] * 8,
            out_specs=[vmem] * 5,
            scratch_shapes=[pltpu.VMEM(x.shape, x.dtype) for x in args]
            + [
                pltpu.VMEM((3, experts, width, LANES), BF16),
                pltpu.VMEM((halves, blocks, units, LANES), F32),
                pltpu.VMEM((rows, units, LANES), F32),
                pltpu.VMEM((halves, blocks, units, LANES), F32),
                pltpu.SemaphoreType.DMA((6, experts)),
                pltpu.SemaphoreType.DMA((2,)),
                pltpu.SemaphoreType.DMA,
                pltpu.SemaphoreType.DMA,
                pltpu.SemaphoreType.DMA,
                pltpu.SemaphoreType.DMA,
                pltpu.SemaphoreType.DMA((3,)),
                pltpu.SemaphoreType.DMA((3,)),
                pltpu.SemaphoreType.DMA,
                pltpu.SemaphoreType.DMA,
                pltpu.SemaphoreType.DMA,
                pltpu.SemaphoreType.DMA,
            ],
            compiler_params=pltpu.CompilerParams(
                collective_id=0, has_side_effects=True, vmem_limit_bytes=44 * 1024 * 1024
            ),
            name="exchange",
        )(*args)
        scale = jax.ShapeDtypeStruct((experts, mine), F32)
        whole = jax.ShapeDtypeStruct((experts, mine, rows * LANES), BF16)
        fg, fu, fd, a, b, c, fr = pl.pallas_call(
            store_kernel,
            out_shape=[whole] * 3 + [scale] * 3 + [jax.ShapeDtypeStruct(ro.shape, BF16)],
            in_specs=[vmem] * 5,
            out_specs=[hbm] * 7,
            scratch_shapes=[pltpu.SemaphoreType.DMA((7,))],
            compiler_params=pltpu.CompilerParams(vmem_limit_bytes=1024 * 1024),
            name="store",
        )(*[pltpu.with_memory_space_constraint(x, pltpu.VMEM) for x in (og, ou, od, sc, ro)])
        fr = fr.reshape(owners * rw.shape[1], rows * LANES)
        return (jnp.swapaxes(fg, 1, 2), jnp.swapaxes(fu, 1, 2), fd, a, b, c, fr.T)

    placed = (
        P("owner", "rows", None),
        P("owner", "rows", None),
        P("owner", "rows", None),
        P("owner", "rows", None),
        P("owner", None, "rows"),
        P("owner", None, "rows"),
        P("rows", "owner"),
        P("rows"),
    )
    return jax.shard_map(
        body,
        mesh=mesh,
        in_specs=placed,
        out_specs=(
            P("owner", None, "rows"),
            P("owner", None, "rows"),
            P("owner", "rows", None),
            P("owner", "rows"),
            P("owner", "rows"),
            P("owner", "rows"),
            P(),
        ),
        check_vma=False,
    )
```

time: 203 us -> 93.7 us (0.46)
  Pallas kernels: 0 us -> 93 us
  waiting for transfers between devices: 76.1 us -> 0 us
  local copies, waits for them, and re-layouts: 38.8 us -> 0 us
  other arithmetic: 32.3 us -> 0 us
  blocking collectives: 29.4 us -> 0 us
  starting transfers between devices: 25.2 us -> 0 us
    pallas_call x0 -> x2, Pallas kernels: none -> 93 us  [the longest x1 90.2 us: body(): pl.pallas_call(functools.partial(exchange_kernel, rows, owners), out_shap...]
    all_to_all x5 -> x0, waiting for transfers between devices: 76.1 us -> none  [the longest x1 54.5 us: side_by_side(): lax.all_to_all(both, axis, split_axis=split_dim, concat_axis=concat_dim,...]
    all_to_all x1 -> x0, blocking collectives: 29.4 us -> none  [sent_to_all(): return lax.all_to_all(copies, axis, split_axis=0, concat_axis=0, tiled=True)]
    all_to_all x5 -> x0, starting transfers between devices: 25.2 us -> none  [the longest x2 12.5 us: sent_to_all(): return lax.all_to_all(copies, axis, split_axis=0, concat_axis=0, tiled=True)]
    unnamed x9 -> x0, local copies, waits for them, and re-layouts: 20 us -> none
    reduce_sum x4 -> x0, other arithmetic: 13.9 us -> none  [the longest x1 4.05 us: body(): jnp.sum(merged_gate * merged_gate, axis=1)]
    convert_element_type x4 -> x0, other arithmetic: 12.8 us -> none  [the longest x1 4.56 us: body(): (merged_gate / jnp.expand_dims(scale_gate, 1)).astype(jnp.bfloat16)]
    split x3 -> x0, local copies, waits for them, and re-layouts: 4.8 us -> none  [several_exchanges(): jnp.split(blocks, piece_ends(blocks.shape[cut], pieces), axis=cut)]
  transfers between devices with their start and end apart: 5 -> 0, of which waited for: 3 -> 0; matrix products, arithmetic and copies ran while one was open for 29% -> 0% of each run, Pallas kernels for 0% -> 0%
where the time goes in v1:
time: 93.7 us; the launch traced here: 93.6 us
  Pallas kernels  93 us (99%)
    pallas_call x1, Pallas kernels, body(): pl.pallas_call(functools.partial(exchange_kernel, rows, owners), out_shap...  90.2 us
    pallas_call x1, Pallas kernels, body(): pl.pallas_call(store_kernel, out_shape=[whole] * 3 + [scale] * 3 + [jax.S...  2.78 us

profile of v1, /device:TPU:0, one launch (start us, length us, event | category | flops | bytes accessed | tf_op | source)
XLA Modules:
  0.0 93.6 jit_solution(10590355469587241736)
XLA Ops:
  0.6 90.2 %exchange.1 = (bf16[8,64,2048]{2,1,0:T(8,128)(2,1)S(1)}, bf16[8,64,2048]{2,1,0:T(8,128)(2,1)S(1)}, bf16[8,64,2048]{2,1,0:T(8,128)(2,1)S(1)}, f32[3,8,64]{2,1,0:T(8,128)S(1)}, bf16[8,8,2048]{2,1,0:T(8,128)(2,1)S(1)}) custom-call(f32[8,128,1024]{2,1,0:T(8,128)} %mg.1, bf16[8,128,1024]{2,1,0:T(8,128)(2,1)} %sg.1, f32[8,128,1024]{2,1,0:T(8,128)} %mu.1, ...), custom_call_target="tpu_custom_call" | custom-call | tf_op jit(solution)/shard_map/exchange/pallas_call | solution.py:224
  90.9 2.8 %store.1 = (bf16[8,64,2048]{2,1,0:T(8,128)(2,1)}, bf16[8,64,2048]{2,1,0:T(8,128)(2,1)}, bf16[8,64,2048]{2,1,0:T(8,128)(2,1)}, f32[8,64]{1,0:T(8,128)}, f32[8,64]...) custom-call(bf16[8,64,2048]{2,1,0:T(8,128)(2,1)S(1)} %get-tuple-element.19.og, ...), custom_call_target="tpu_custom_call" | custom-call | tf_op jit(solution)/shard_map/store/pallas_call | solution.py:259

commit v2 on v1

v2 whole, which is shorter than its diff:
```python
import functools

import jax
import jax.numpy as jnp
from jax import lax
from jax.experimental import pallas as pl
from jax.experimental.pallas import tpu as pltpu
from jax.sharding import PartitionSpec as P

F32 = jnp.float32
BF16 = jnp.bfloat16
MESH = pl.DeviceIdType.MESH
Y = 4
LANES = 128


FIRST = 2
CORES = 2


def exchange_kernel(
    rows,
    owners,
    mg, sg, mu, su, md, sd, rw, gain,
    og, ou, od, sc, ro,
    vmg, vsg, vmu, vsu, vmd, vsd, vrw, vgain,
    send, early, tot, part_b, part_c, got_b, got_c, sum_b, sum_c,
    in_sem, small_sem, stat_send, stat_recv,
    data_send, data_recv, row_send, row_recv, own_send, own_recv, half_send, half_recv,
):
    experts = mg.shape[0]
    width = mg.shape[2]
    blocks = width // LANES
    mine = width // rows
    halves = rows // blocks
    share = LANES // mine
    owner = lax.axis_index("owner")
    me = lax.axis_index("rows")
    z, y = me // Y, me % Y
    peers = [((z + k // Y) % (rows // Y)) * Y + (y + k % Y) % Y for k in range(1, rows)]
    core = owner % CORES
    others = [(owner + k) % owners for k in range(CORES, owners, CORES)]
    partner = owner + 1 - 2 * core
    lanes = pl.ds(pl.multiple_of(me * LANES, LANES), LANES)

    barrier = pltpu.get_barrier_semaphore()
    for p in peers:
        pl.semaphore_signal(barrier, inc=1, device_id={"rows": p}, device_id_type=MESH)
    for p in others:
        pl.semaphore_signal(barrier, inc=1, device_id={"owner": p}, device_id_type=MESH)

    @pl.when(core == 0)
    def _():
        pl.semaphore_signal(barrier, inc=1, device_id={"owner": partner}, device_id_type=MESH)

    matrices = (
        (mg, sg, vmg, vsg, og, True),
        (mu, su, vmu, vsu, ou, True),
        (md, sd, vmd, vsd, od, False),
    )

    def loads(m, e):
        master, second, vm, vs = matrices[m][:4]
        return (
            pltpu.make_async_copy(master.at[e], vm.at[e], in_sem.at[2 * m, e]),
            pltpu.make_async_copy(second.at[e], vs.at[e], in_sem.at[2 * m + 1, e]),
        )

    small = (
        pltpu.make_async_copy(rw, vrw, small_sem.at[0]),
        pltpu.make_async_copy(gain, vgain, small_sem.at[1]),
    )
    for m in range(3):
        @pl.loop(0, experts)
        def _(e):
            for c in loads(m, e):
                c.start()
    for c in small:
        c.start()

    def block(b):
        return slice(b * LANES, (b + 1) * LANES)

    def partial_sums(m, e):
        vm, vs, across = matrices[m][2], matrices[m][3], matrices[m][5]
        for c in loads(m, e):
            c.wait()
        if across:
            acc = jnp.zeros((8, width), F32)
            for i in range(0, vm.shape[1], 16):
                x = vm[e, i : i + 16, :] + vs[e, i : i + 16, :].astype(F32)
                x = x * x
                acc = acc + x[:8] + x[8:]
            total = jnp.sum(acc, axis=0, keepdims=True)
            return [total[:, block(b)] for b in range(blocks)]
        result = []
        for b in range(blocks):
            x = vm[e, block(b), :] + vs[e, block(b), :].astype(F32)
            result.append(jnp.sum((x * x).T, axis=0, keepdims=True))
        return result

    def ship(m, e, totals):
        vm, vs, out, across = matrices[m][2], matrices[m][3], matrices[m][4], matrices[m][5]
        for j in range(blocks):
            b = (me // share + j) % blocks
            at = pl.ds(pl.multiple_of(b * LANES, LANES), LANES)
            inverse = 1.0 / jnp.sqrt(totals(b))
            if across:
                x = (vm[e, :, at] + vs[e, :, at].astype(F32)) * inverse
                send[m, e, at, :] = x.T.astype(BF16)
            else:
                x = vm[e, at, :] + vs[e, at, :].astype(F32)
                send[m, e, at, :] = (x * jnp.broadcast_to(inverse, (LANES, LANES)).T).astype(BF16)
            for k in range(share) if j else range(1, share):
                p = b * share + (me + k) % share
                pltpu.make_async_remote_copy(
                    src_ref=send.at[m, e, pl.ds(pl.multiple_of(p * mine, mine), mine)],
                    dst_ref=out.at[e, :, lanes],
                    send_sem=data_send.at[m], recv_sem=data_recv.at[m],
                    device_id={"rows": p}, device_id_type=MESH,
                ).start()
        out[e, :, lanes] = send[m, e, pl.ds(pl.multiple_of(me * mine, mine), mine), :]

    def to_peers(src, dst, at):
        for p in peers:
            pltpu.make_async_remote_copy(
                src_ref=src(p), dst_ref=dst, send_sem=stat_send.at[at], recv_sem=stat_recv.at[at],
                device_id={"rows": p}, device_id_type=MESH,
            ).start()

    def arrived(ref, sem):
        shares = ref.at[pl.ds(0, rows - 1)]
        pltpu.make_async_copy(shares, shares, sem).wait()

    @pl.loop(0, FIRST)
    def _(e):
        for b, row in enumerate(partial_sums(0, e)):
            early[me, e, b : b + 1, :] = row

    pl.semaphore_wait(barrier, rows - 1 + len(others) + core)
    to_peers(lambda p: early.at[me], early.at[me], 0)

    @pl.loop(FIRST, experts)
    def _(e):
        for b, row in enumerate(partial_sums(0, e)):
            part_b[(e - FIRST) % halves, b, (e - FIRST) // halves] = row

    to_peers(lambda p: part_b.at[p // blocks, p % blocks], got_b.at[me], 1)
    got_b[me] = part_b[me // blocks, me % blocks]

    for c in small:
        c.wait()
    ro[core, owner // CORES, :, lanes] = (vrw[...] * vgain[...]).astype(BF16)
    for p in peers:
        pltpu.make_async_remote_copy(
            src_ref=ro.at[core, owner // CORES, :, lanes], dst_ref=ro.at[core, owner // CORES, :, lanes],
            send_sem=row_send, recv_sem=row_recv, device_id={"rows": p}, device_id_type=MESH,
        ).start()

    @pl.loop(0, experts)
    def _(e):
        for b, row in enumerate(partial_sums(1, e)):
            part_c[e % halves, b, e // halves] = row

    arrived(early, stat_recv.at[0])
    total = early[0]
    for k in range(1, rows):
        total = total + early[k]
    tot[...] = total

    def early_totals(e):
        return lambda b: tot[e, pl.ds(b, 1), :]

    def stage_totals(ref, at):
        return lambda b: ref[(at % halves) * blocks + b, at // halves]

    ship(0, 0, early_totals(0))

    def add_up(got, whole, at):
        arrived(got, stat_recv.at[at])
        total = got[0]
        for k in range(1, rows):
            total = total + got[k]
        whole[me] = total
        to_peers(lambda p: whole.at[me], whole.at[me], at + 1)

    add_up(got_b, sum_b, 1)

    @pl.loop(1, FIRST)
    def _(e):
        ship(0, e, early_totals(e))

    @pl.loop(0, experts)
    def _(e):
        for b, row in enumerate(partial_sums(2, e)):
            part_c[e % halves, b, (experts + e) // halves] = row

    to_peers(lambda p: part_c.at[p // blocks, p % blocks], got_c.at[me], 3)
    got_c[me] = part_c[me // blocks, me % blocks]

    arrived(sum_b, stat_recv.at[2])

    def ship_gate(e):
        ship(0, e, stage_totals(sum_b, e - FIRST))

    pl.loop(FIRST, experts - 2)(ship_gate)
    add_up(got_c, sum_c, 3)
    pl.loop(experts - 2, experts)(ship_gate)

    row = ro.at[core, owner // CORES, :, pl.ds(0, (rows - 1) * LANES)]
    pltpu.make_async_copy(row, row, row_recv).wait()
    pltpu.make_async_copy(row, row, row_send).wait()
    for p in others:
        pltpu.make_async_remote_copy(
            src_ref=ro.at[core, owner // CORES], dst_ref=ro.at[core, owner // CORES],
            send_sem=own_send, recv_sem=own_recv, device_id={"owner": p}, device_id_type=MESH,
        ).start()

    def ship_rest(m):
        @pl.loop(0, experts)
        def _(e):
            ship(m, e, stage_totals(sum_c, (m - 1) * experts + e))

    arrived(sum_c, stat_recv.at[4])
    ship_rest(1)

    theirs = ro.at[core, pl.ds(0, owners // CORES - 1)]
    pltpu.make_async_copy(theirs, theirs, own_send).wait()
    pltpu.make_async_copy(theirs, theirs, own_recv).wait()
    half = pltpu.make_async_remote_copy(
        src_ref=ro.at[core], dst_ref=ro.at[core],
        send_sem=half_send, recv_sem=half_recv, device_id={"owner": partner}, device_id_type=MESH,
    )

    @pl.when(core == 1)
    def _():
        half.start()

    @pl.when(core == 0)
    def _():
        half.wait_recv()
        half.start()

    ship_rest(2)

    def own_scale(value):
        value = jnp.sqrt(value)
        value = jnp.where(me % 2 == 1, pltpu.roll(value, LANES - mine, 1), value)
        return value[:, :mine]

    pair = me // 2
    for e in range(FIRST):
        sc[0, e : e + 1, :] = own_scale(tot[e, pl.ds(pair, 1), :])
    for u in range(3 * experts - FIRST):
        m, e = (u + FIRST) // experts, (u + FIRST) % experts
        ref, at = (sum_b, u) if m == 0 else (sum_c, u + FIRST - experts)
        sc[m, e : e + 1, :] = own_scale(ref[(at % halves) * blocks + pair, at // halves])

    for at, ref in enumerate((early, got_b, sum_b, got_c, sum_c)):
        arrived(ref, stat_send.at[at])
    half.wait_send()

    @pl.when(core == 1)
    def _():
        half.wait_recv()

    for m in range(3):
        sent = send.at[m, :, pl.ds(0, (rows - 1) * mine), :]
        pltpu.make_async_copy(sent, sent, data_send.at[m]).wait()
        pltpu.make_async_copy(sent, sent, data_recv.at[m]).wait()


def store_kernel(og, ou, od, sc, ro, fg, fu, fd, a, b, c, fr, sem):
    copies = [
        pltpu.make_async_copy(og, fg, sem.at[0]),
        pltpu.make_async_copy(ou, fu, sem.at[1]),
        pltpu.make_async_copy(od, fd, sem.at[2]),
        pltpu.make_async_copy(ro.at[0], fr.at[:, 0], sem.at[3]),
        pltpu.make_async_copy(ro.at[1], fr.at[:, 1], sem.at[7]),
        pltpu.make_async_copy(sc.at[0], a, sem.at[4]),
        pltpu.make_async_copy(sc.at[1], b, sem.at[5]),
        pltpu.make_async_copy(sc.at[2], c, sem.at[6]),
    ]
    for copy in copies:
        copy.start()
    for copy in copies:
        copy.wait()


def solution(mesh):
    owners, rows = mesh.shape["owner"], mesh.shape["rows"]

    def body(mg, sg, mu, su, md, sd, rw, gain):
        experts, deep, width = mg.shape
        blocks = width // LANES
        halves = rows // blocks
        units_b = (experts - FIRST) // halves
        units_c = 2 * experts // halves
        mine = width // rows
        hbm = pl.BlockSpec(memory_space=pltpu.HBM)
        vmem = pl.BlockSpec(memory_space=pltpu.VMEM)
        result = pltpu.VMEM((experts, mine, rows * LANES), BF16)
        args = [mg, sg, mu, su, md, sd, rw.T, gain[None, :]]
        args = [pltpu.with_memory_space_constraint(x, pltpu.HBM) for x in args]
        og, ou, od, sc, ro = pl.pallas_call(
            functools.partial(exchange_kernel, rows, owners),
            out_shape=[
                result, result, result,
                pltpu.VMEM((3, experts, mine), F32),
                pltpu.VMEM((CORES, owners // CORES, rw.shape[1], rows * LANES), BF16),
            ],
            in_specs=[hbm] * 8,
            out_specs=[vmem] * 5,
            scratch_shapes=[pltpu.VMEM(x.shape, x.dtype) for x in args]
            + [
                pltpu.VMEM((3, experts, width, LANES), BF16),
                pltpu.VMEM((rows, FIRST, blocks, LANES), F32),
                pltpu.VMEM((FIRST, blocks, LANES), F32),
                pltpu.VMEM((halves, blocks, units_b, 1, LANES), F32),
                pltpu.VMEM((halves, blocks, units_c, 1, LANES), F32),
                pltpu.VMEM((rows, units_b, 1, LANES), F32),
                pltpu.VMEM((rows, units_c, 1, LANES), F32),
                pltpu.VMEM((rows, units_b, 1, LANES), F32),
                pltpu.VMEM((rows, units_c, 1, LANES), F32),
                pltpu.SemaphoreType.DMA((6, experts)),
                pltpu.SemaphoreType.DMA((2,)),
                pltpu.SemaphoreType.DMA((5,)),
                pltpu.SemaphoreType.DMA((5,)),
                pltpu.SemaphoreType.DMA((3,)),
                pltpu.SemaphoreType.DMA((3,)),
                pltpu.SemaphoreType.DMA,
                pltpu.SemaphoreType.DMA,
                pltpu.SemaphoreType.DMA,
                pltpu.SemaphoreType.DMA,
                pltpu.SemaphoreType.DMA,
                pltpu.SemaphoreType.DMA,
            ],
            compiler_params=pltpu.CompilerParams(
                collective_id=0, has_side_effects=True, vmem_limit_bytes=44 * 1024 * 1024
            ),
            name="exchange",
        )(*args)
        scale = jax.ShapeDtypeStruct((experts, mine), F32)
        whole = jax.ShapeDtypeStruct((experts, mine, rows * LANES), BF16)
        fg, fu, fd, a, b, c, fr = pl.pallas_call(
            store_kernel,
            out_shape=[whole] * 3 + [scale] * 3 + [jax.ShapeDtypeStruct((owners // CORES, CORES, *ro.shape[2:]), BF16)],
            in_specs=[vmem] * 5,
            out_specs=[hbm] * 7,
            scratch_shapes=[pltpu.SemaphoreType.DMA((8,))],
            compiler_params=pltpu.CompilerParams(vmem_limit_bytes=1024 * 1024),
            name="store",
        )(*[pltpu.with_memory_space_constraint(x, pltpu.VMEM) for x in (og, ou, od, sc, ro)])
        fr = fr.reshape(owners * rw.shape[1], rows * LANES)
        return (jnp.swapaxes(fg, 1, 2), jnp.swapaxes(fu, 1, 2), fd, a, b, c, fr.T)

    placed = (
        P("owner", "rows", None),
        P("owner", "rows", None),
        P("owner", "rows", None),
        P("owner", "rows", None),
        P("owner", None, "rows"),
        P("owner", None, "rows"),
        P("rows", "owner"),
        P("rows"),
    )
    return jax.shard_map(
        body,
        mesh=mesh,
        in_specs=placed,
        out_specs=(
            P("owner", None, "rows"),
            P("owner", None, "rows"),
            P("owner", "rows", None),
            P("owner", "rows"),
            P("owner", "rows"),
            P("owner", "rows"),
            P(),
        ),
        check_vma=False,
    )
```

time: 93.7 us -> 87.4 us (0.933)
  Pallas kernels: 93 us -> 86.6 us
    pallas_call x1, Pallas kernels: 90.2 us -> 83.9 us  [body(): pl.pallas_call(functools.partial(exchange_kernel, rows, owners), out_shap...]
where the time goes in v2:
time: 87.4 us; the launch traced here: 87.3 us
  Pallas kernels  86.6 us (99%)
    pallas_call x1, Pallas kernels, body(): pl.pallas_call(functools.partial(exchange_kernel, rows, owners), out_shap...  83.9 us
    pallas_call x1, Pallas kernels, body(): pl.pallas_call(store_kernel, out_shape=[whole] * 3 + [scale] * 3 + [jax.S...  2.78 us

profile of v2, /device:TPU:0, one launch (start us, length us, event | category | flops | bytes accessed | tf_op | source)
XLA Modules:
  0.0 87.3 jit_solution(11873935643232238153)
XLA Ops:
  0.6 83.9 %exchange.1 = (bf16[8,64,2048]{2,1,0:T(8,128)(2,1)S(1)}, bf16[8,64,2048]{2,1,0:T(8,128)(2,1)S(1)}, bf16[8,64,2048]{2,1,0:T(8,128)(2,1)S(1)}, f32[3,8,64]{2,1,0:T(8,128)S(1)}, bf16[2,4,8,2048]{3,2,1,0:T(8,128)(2,1)S(1)}) custom-call(f32[8,128,1024]{2,1,0:T(8,128)} %mg.1, bf16[8,128,1024]{2,1,0:T(8,128)(2,1)} %sg.1, f32[8,128,1024]{2,1,0:T(8,128)} %mu.1, ...), custom_call_target="tpu_custom_call" | custom-call | tf_op jit(solution)/shard_map/exchange/pallas_call | solution.py:305
  84.5 2.8 %store.1 = (bf16[8,64,2048]{2,1,0:T(8,128)(2,1)}, bf16[8,64,2048]{2,1,0:T(8,128)(2,1)}, bf16[8,64,2048]{2,1,0:T(8,128)(2,1)}, f32[8,64]{1,0:T(8,128)}, f32[8,64]...) custom-call(bf16[8,64,2048]{2,1,0:T(8,128)(2,1)S(1)} %get-tuple-element.19.og, ...), custom_call_target="tpu_custom_call" | custom-call | tf_op jit(solution)/shard_map/store/pallas_call | solution.py:345

commit v3 on v2

--- a/solution.py
+++ b/solution.py
@@ -15,6 +15,7 @@
 
 
 FIRST = 2
+PLAIN = 32
 CORES = 2
 
 
@@ -24,9 +25,9 @@
     mg, sg, mu, su, md, sd, rw, gain,
     og, ou, od, sc, ro,
     vmg, vsg, vmu, vsu, vmd, vsd, vrw, vgain,
-    send, early, tot, part_b, part_c, got_b, got_c, sum_b, sum_c,
+    send, plain, landed, spread, early, tot, part_b, part_c, got_b, got_c, sum_b, sum_c,
     in_sem, small_sem, stat_send, stat_recv,
-    data_send, data_recv, row_send, row_recv, own_send, own_recv, half_send, half_recv,
+    data_send, data_recv, plain_send, plain_recv, row_send, row_recv, own_send, own_recv, half_send, half_recv,
 ):
     experts = mg.shape[0]
     width = mg.shape[2]
@@ -70,20 +71,25 @@
         pltpu.make_async_copy(rw, vrw, small_sem.at[0]),
         pltpu.make_async_copy(gain, vgain, small_sem.at[1]),
     )
-    for m in range(3):
-        @pl.loop(0, experts)
+
+    def start_loads(m, lo, hi):
+        @pl.loop(lo, hi)
         def _(e):
             for c in loads(m, e):
                 c.start()
+
+    start_loads(0, 0, FIRST)
+    start_loads(2, experts - 1, experts)
+    start_loads(0, FIRST, experts)
     for c in small:
         c.start()
 
     def block(b):
         return slice(b * LANES, (b + 1) * LANES)
 
-    def partial_sums(m, e):
+    def partial_sums(m, e, wait=True):
         vm, vs, across = matrices[m][2], matrices[m][3], matrices[m][5]
-        for c in loads(m, e):
+        for c in loads(m, e) if wait else ():
             c.wait()
         if across:
             acc = jnp.zeros((8, width), F32)
@@ -99,7 +105,9 @@
             result.append(jnp.sum((x * x).T, axis=0, keepdims=True))
         return result
 
-    def ship(m, e, totals):
+    last = experts - 1
+
+    def ship(m, e, totals, skip=0):
         vm, vs, out, across = matrices[m][2], matrices[m][3], matrices[m][4], matrices[m][5]
         for j in range(blocks):
             b = (me // share + j) % blocks
@@ -114,12 +122,12 @@
             for k in range(share) if j else range(1, share):
                 p = b * share + (me + k) % share
                 pltpu.make_async_remote_copy(
-                    src_ref=send.at[m, e, pl.ds(pl.multiple_of(p * mine, mine), mine)],
-                    dst_ref=out.at[e, :, lanes],
-                    send_sem=data_send.at[m], recv_sem=data_recv.at[m],
+                    src_ref=send.at[m, e, pl.ds(pl.multiple_of(p * mine + skip, 16), mine - skip)],
+                    dst_ref=out.at[e, skip:, lanes],
+                    send_sem=data_send.at[m + (skip > 0)], recv_sem=data_recv.at[m + (skip > 0)],
                     device_id={"rows": p}, device_id_type=MESH,
                 ).start()
-        out[e, :, lanes] = send[m, e, pl.ds(pl.multiple_of(me * mine, mine), mine), :]
+        out[e, skip:, lanes] = send[m, e, pl.ds(pl.multiple_of(me * mine + skip, 16), mine - skip), :]
 
     def to_peers(src, dst, at):
         for p in peers:
@@ -147,6 +155,36 @@
 
     to_peers(lambda p: part_b.at[p // blocks, p % blocks], got_b.at[me], 1)
     got_b[me] = part_b[me // blocks, me % blocks]
+
+    for c in loads(2, last):
+        c.wait()
+
+    @pl.loop(0, rows)
+    def _(p):
+        at = pl.ds(pl.multiple_of(p * mine, mine), PLAIN)
+        plain[p] = vmd[last, at, :] + vsd[last, at, :].astype(F32)
+
+    for p in peers:
+        pltpu.make_async_remote_copy(
+            src_ref=plain.at[p], dst_ref=landed.at[me], send_sem=plain_send, recv_sem=plain_recv,
+            device_id={"rows": p}, device_id_type=MESH,
+        ).start()
+    landed[me] = plain[me]
+    start_loads(1, 0, experts)
+
+    arrived(early, stat_recv.at[0])
+    total = early[0]
+    for k in range(1, rows):
+        total = total + early[k]
+    tot[...] = total
+
+    def early_totals(e):
+        return lambda b: tot[e, pl.ds(b, 1), :]
+
+    def stage_totals(ref, at):
+        return lambda b: ref[(at % halves) * blocks + b, at // halves]
+
+    ship(0, 0, early_totals(0))
 
     for c in small:
         c.wait()
@@ -157,25 +195,6 @@
             send_sem=row_send, recv_sem=row_recv, device_id={"rows": p}, device_id_type=MESH,
         ).start()
 
-    @pl.loop(0, experts)
-    def _(e):
-        for b, row in enumerate(partial_sums(1, e)):
-            part_c[e % halves, b, e // halves] = row
-
-    arrived(early, stat_recv.at[0])
-    total = early[0]
-    for k in range(1, rows):
-        total = total + early[k]
-    tot[...] = total
-
-    def early_totals(e):
-        return lambda b: tot[e, pl.ds(b, 1), :]
-
-    def stage_totals(ref, at):
-        return lambda b: ref[(at % halves) * blocks + b, at // halves]
-
-    ship(0, 0, early_totals(0))
-
     def add_up(got, whole, at):
         arrived(got, stat_recv.at[at])
         total = got[0]
@@ -190,10 +209,20 @@
     def _(e):
         ship(0, e, early_totals(e))
 
+    start_loads(2, 0, last)
+
     @pl.loop(0, experts)
+    def _(e):
+        for b, row in enumerate(partial_sums(1, e)):
+            part_c[e % halves, b, e // halves] = row
+
+    @pl.loop(0, last)
     def _(e):
         for b, row in enumerate(partial_sums(2, e)):
             part_c[e % halves, b, (experts + e) // halves] = row
+
+    for b, row in enumerate(partial_sums(2, last, False)):
+        part_c[last % halves, b, (experts + last) // halves] = row
 
     to_peers(lambda p: part_c.at[p // blocks, p % blocks], got_c.at[me], 3)
     got_c[me] = part_c[me // blocks, me % blocks]
@@ -216,13 +245,11 @@
             send_sem=own_send, recv_sem=own_recv, device_id={"owner": p}, device_id_type=MESH,
         ).start()
 
-    def ship_rest(m):
-        @pl.loop(0, experts)
-        def _(e):
-            ship(m, e, stage_totals(sum_c, (m - 1) * experts + e))
+    def ship_rest(m, lo, hi, skip=0):
+        pl.loop(lo, hi)(lambda e: ship(m, e, stage_totals(sum_c, (m - 1) * experts + e), skip))
 
     arrived(sum_c, stat_recv.at[4])
-    ship_rest(1)
+    ship_rest(1, 0, experts)
 
     theirs = ro.at[core, pl.ds(0, owners // CORES - 1)]
     pltpu.make_async_copy(theirs, theirs, own_send).wait()
@@ -241,7 +268,15 @@
         half.wait_recv()
         half.start()
 
-    ship_rest(2)
+    ship_rest(2, 0, last)
+    ship_rest(2, last, experts, PLAIN)
+
+    inverse = 1.0 / jnp.sqrt(stage_totals(sum_c, experts + last)(me // share))
+    spread[...] = jnp.broadcast_to(inverse, (LANES, LANES)).T
+    scale = spread[pl.ds(pl.multiple_of((me % share) * mine, mine), PLAIN), :]
+    arrived(landed, plain_recv)
+    for k in range(rows):
+        od[last, :PLAIN, k * LANES : (k + 1) * LANES] = (landed[k] * scale).astype(BF16)
 
     def own_scale(value):
         value = jnp.sqrt(value)
@@ -264,8 +299,14 @@
     def _():
         half.wait_recv()
 
-    for m in range(3):
-        sent = send.at[m, :, pl.ds(0, (rows - 1) * mine), :]
+    arrived(landed, plain_send)
+    for m in range(4):
+        if m < 2:
+            sent = send.at[m, :, pl.ds(0, (rows - 1) * mine), :]
+        elif m == 2:
+            sent = send.at[m, pl.ds(0, last), pl.ds(0, (rows - 1) * mine), :]
+        else:
+            sent = send.at[2, last, pl.ds(0, (rows - 1) * (mine - PLAIN)), :]
         pltpu.make_async_copy(sent, sent, data_send.at[m]).wait()
         pltpu.make_async_copy(sent, sent, data_recv.at[m]).wait()
 
@@ -314,6 +355,9 @@
             scratch_shapes=[pltpu.VMEM(x.shape, x.dtype) for x in args]
             + [
                 pltpu.VMEM((3, experts, width, LANES), BF16),
+                pltpu.VMEM((rows, PLAIN, LANES), F32),
+                pltpu.VMEM((rows, PLAIN, LANES), F32),
+                pltpu.VMEM((LANES, LANES), F32),
                 pltpu.VMEM((rows, FIRST, blocks, LANES), F32),
                 pltpu.VMEM((FIRST, blocks, LANES), F32),
                 pltpu.VMEM((halves, blocks, units_b, 1, LANES), F32),
@@ -326,8 +370,10 @@
                 pltpu.SemaphoreType.DMA((2,)),
                 pltpu.SemaphoreType.DMA((5,)),
                 pltpu.SemaphoreType.DMA((5,)),
-                pltpu.SemaphoreType.DMA((3,)),
-                pltpu.SemaphoreType.DMA((3,)),
+                pltpu.SemaphoreType.DMA((4,)),
+                pltpu.SemaphoreType.DMA((4,)),
+                pltpu.SemaphoreType.DMA,
+                pltpu.SemaphoreType.DMA,
                 pltpu.SemaphoreType.DMA,
                 pltpu.SemaphoreType.DMA,
                 pltpu.SemaphoreType.DMA,

time: 87.4 us -> 86.8 us (level)
  no operation moved by 1% of the time
where the time goes in v3:
time: 86.8 us; the launch traced here: 86.7 us
  Pallas kernels  86 us (99%)
    pallas_call x1, Pallas kernels, body(): pl.pallas_call(functools.partial(exchange_kernel, rows, owners), out_shap...  83.2 us
    pallas_call x1, Pallas kernels, body(): pl.pallas_call(store_kernel, out_shape=[whole] * 3 + [scale] * 3 + [jax.S...  2.78 us

profile of v3, /device:TPU:0, one launch (start us, length us, event | category | flops | bytes accessed | tf_op | source)
XLA Modules:
  0.0 86.7 jit_solution(8283175878678032134)
XLA Ops:
  0.6 83.2 %exchange.1 = (bf16[8,64,2048]{2,1,0:T(8,128)(2,1)S(1)}, bf16[8,64,2048]{2,1,0:T(8,128)(2,1)S(1)}, bf16[8,64,2048]{2,1,0:T(8,128)(2,1)S(1)}, f32[3,8,64]{2,1,0:T(8,128)S(1)}, bf16[2,4,8,2048]{3,2,1,0:T(8,128)(2,1)S(1)}) custom-call(f32[8,128,1024]{2,1,0:T(8,128)} %mg.1, bf16[8,128,1024]{2,1,0:T(8,128)(2,1)} %sg.1, f32[8,128,1024]{2,1,0:T(8,128)} %mu.1, ...), custom_call_target="tpu_custom_call" | custom-call | tf_op jit(solution)/shard_map/exchange/pallas_call | solution.py:346
  83.9 2.8 %store.1 = (bf16[8,64,2048]{2,1,0:T(8,128)(2,1)}, bf16[8,64,2048]{2,1,0:T(8,128)(2,1)}, bf16[8,64,2048]{2,1,0:T(8,128)(2,1)}, f32[8,64]{1,0:T(8,128)}, f32[8,64]...) custom-call(bf16[8,64,2048]{2,1,0:T(8,128)(2,1)S(1)} %get-tuple-element.19.og, ...), custom_call_target="tpu_custom_call" | custom-call | tf_op jit(solution)/shard_map/store/pallas_call | solution.py:391
